TPU v7x, 32 devices: a whole 2x2x4 slice. The times are simulated.
32 devices in a mesh: rows: 4 (over x, core), cols: 4 (over z), slabs: 2 (over y).
Axes of the slice: x: 2, y: 2, z: 4, core: 2. Of those that a mesh axis runs over, the one named last changes fastest.
Arguments:
- pressure: float32 [64, 32, 256, 128], P('rows', 'cols', 'slabs'), may hold values from 0.2 to 1.8
- earlier: float32 [64, 32, 256, 128], P('rows', 'cols', 'slabs'), may hold values from 0.2 to 1.8
- speed_square: float32 [64, 32, 256, 128], P('rows', 'cols', 'slabs'), may hold values from 0.05 to 0.3
Outputs:
- column_sum: float32 [64, 32, 256, 128], P('rows', 'cols', 'slabs')
- pressure_end: float32 [64, 32, 256, 128], P('rows', 'cols', 'slabs')
All inputs are finite; a program needn't handle non-finite values.
Results may differ from a plain program's by a relative error of at most 0.00002.
Values sent between devices are 32-bit elements; how exact they have to be, the bound alone decides.
A program may use at most 128 MiB of HBM per device.

v0:
```python
import jax
import jax.numpy as jnp
from jax import lax
from jax.sharding import PartitionSpec as P

STEPS = 6


def padded_2(x, sides, width):
    for axis, dim in sides:
        count, length = (lax.axis_size(axis), x.shape[dim])
        up = [(i, (i + 1) % count) for i in range(count - 1)]
        down = [(j, i) for i, j in up]
        last = lax.slice_in_dim(x, length - width, length, axis=dim)
        initial = lax.slice_in_dim(x, 0, width, axis=dim)
        before = lax.ppermute(last, axis, up)
        after = lax.ppermute(initial, axis, down)
        x = jnp.concatenate([before, x, after], axis=dim)
    return x


def prefix(value, axis, join, neutral):
    count, mine = (lax.axis_size(axis), lax.axis_index(axis))
    pieces = lax.all_gather(value, axis)
    so_far = jnp.full_like(value, 0) + jnp.asarray(neutral, value.dtype)

    def turn(position, so_far):
        longer = join(so_far, pieces[position])
        return jnp.where(position < mine, longer, so_far)

    return lax.fori_loop(0, count - 1, turn, so_far)


def inner_cells(values, dims):
    for dim in dims:
        values = lax.slice_in_dim(values, 1, values.shape[dim] - 1, axis=dim)
    return values


def side_cells(values, dim, start, dims):
    others = [other for other in dims if other != dim]
    values = inner_cells(values, others)
    return lax.slice_in_dim(values, start, start + values.shape[dim] - 2, axis=dim)


def advance(padded, before, speed_square):
    middle = inner_cells(padded, (0, 1, 2))
    lower = [side_cells(padded, dim, 0, (0, 1, 2)) for dim in (0, 1, 2)]
    upper = [side_cells(padded, dim, 2, (0, 1, 2)) for dim in (0, 1, 2)]
    spread = lower[0] + upper[0] + lower[1] + upper[1] + lower[2] + upper[2] - 6.0 * middle
    return 2.0 * middle - before + speed_square * spread


def on_device(pressure, earlier, speed_square):
    for step in range(STEPS):
        padded = padded_2(pressure, (("rows", 0), ("cols", 1), ("slabs", 2)), 1)
        later = advance(padded, earlier, speed_square)
        earlier, pressure = (pressure, later)
    here = jnp.cumsum(pressure, axis=1)
    total = lax.slice_in_dim(here, here.shape[1] - 1, here.shape[1], axis=1)

    def add_pair(earlier_total, later_total):
        return earlier_total + later_total

    below = prefix(total, "cols", add_pair, jnp.zeros_like(total))
    column_sum = (here + below) / (pressure.shape[1] * lax.axis_size("cols"))
    return (column_sum, pressure)


def solution(mesh):
    return jax.shard_map(
        on_device,
        mesh=mesh,
        in_specs=(
            P("rows", "cols", "slabs", None),
            P("rows", "cols", "slabs", None),
            P("rows", "cols", "slabs", None),
        ),
        out_specs=(P("rows", "cols", "slabs", None), P("rows", "cols", "slabs", None)),
        check_vma=False,
    )
```

profile of v0, /device:TPU:24, one launch (start us, length us, event | category | flops | bytes accessed | tf_op | source)
XLA Modules:
  0.0 602.0 jit_solution(406570555972608837)
XLA Ops:
  23.5 19.1 %collective-permute-done.2 = f32[18,1,128,128]{3,2,1,0:T(8,128)S(1)} collective-permute-done((f32[18,1,128,128]{3,2,1,0:T(8,128)S(1)}, f32[18,1,128,128]{3,2,1,0:T(8,128)S(1)}, u32[]{:S(2)}, u32[]{:S(2)}) %collective-permute-start.2) | collective-permute-done | bytes 1179680 | tf_op jit(solution)/shard_map/ppermute | solution.py:16
  55.1 28.2 %fusion.43 = f32[16,8,128,128]{3,2,1,0:T(8,128)} fusion(f32[16,8,128,128]{3,2,1,0:T(8,128)S(1)} %bitcast.10, f32[18,10,1,128]{3,2,1,0:T(1,128)S(1)} %copy.29, f32[18,1,128,128]{3,2,1,0:T(8,128)} %copy-done.6, f32[18,8,128,128]{3,2,1,0:T(8,128)} %copy-done.5, f32[18,1,128,128]{3,2,1,0:T(8,128)S(1)} %collective-permute-done.2, ...), kind=kLoop, calls=%fused_computation.135 | loop fusion | flops 44040192 | bytes 46583808 | tf_op jit(solution)/shard_map/add | solution.py:51
  84.8 6.1 %collective-permute-start.6 = (f32[1,8,128,128]{3,2,1,0:T(8,128)S(1)}, f32[1,8,128,128]{3,2,1,0:T(8,128)S(1)}, u32[]{:S(2)}, u32[]{:S(2)}) collective-permute-start(f32[1,8,128,128]{3,2,1,0:T(8,128)S(1)} %get-tuple-element.151), channel_id=1, source_target_pairs={{0,8},{8,16},{16,24},{1,9},{9,17},{17,25},{2,10},{10,18},{18,26},{... | collective-permute-start | bytes 1572872 | tf_op jit(solution)/shard_map/ppermute | solution.py:16
  100.1 5.1 collective-permute-start.9
  105.2 18.0 %collective-permute-done.8 = f32[18,1,128,128]{3,2,1,0:T(8,128)S(1)} collective-permute-done((f32[18,1,128,128]{3,2,1,0:T(8,128)S(1)}, f32[18,1,128,128]{3,2,1,0:T(8,128)S(1)}, u32[]{:S(2)}, u32[]{:S(2)}) %collective-permute-start.8) | collective-permute-done | bytes 1179680 | tf_op jit(solution)/shard_map/ppermute | solution.py:16
  133.5 30.7 %fusion.35 = f32[16,8,128,128]{3,2,1,0:T(8,128)} fusion(f32[16,8,128,128]{3,2,1,0:T(8,128)} %param.7, f32[18,10,1,128]{3,2,1,0:T(1,128)S(1)} %copy.33, f32[18,1,128,128]{3,2,1,0:T(8,128)S(1)} %collective-permute-done.9, f32[18,1,128,128]{3,2,1,0:T(8,128)S(1)} %collective-permute-done.8, f32[1,8,128,128]{3,2,1,0:T(8,128)S(1)} %collective-permute-done.7, ...), kind=kLoop, calls=%fused_computation.109 | loop fusion | flops 60817408 | bytes 37146624 | tf_op jit(solution)/shard_map/add | solution.py:51
  165.7 7.5 %collective-permute-start.12 = (f32[1,8,128,128]{3,2,1,0:T(8,128)S(1)}, f32[1,8,128,128]{3,2,1,0:T(8,128)S(1)}, u32[]{:S(2)}, u32[]{:S(2)}) collective-permute-start(f32[1,8,128,128]{3,2,1,0:T(8,128)S(1)} %get-tuple-element.149), channel_id=1, source_target_pairs={{0,8},{8,16},{16,24},{1,9},{9,17},{17,25},{2,10},{10,18},{18,26},{... | collective-permute-start | bytes 1572872 | tf_op jit(solution)/shard_map/ppermute | solution.py:16
  180.4 5.1 collective-permute-start.15
  185.4 18.0 %collective-permute-done.14 = f32[18,1,128,128]{3,2,1,0:T(8,128)S(1)} collective-permute-done((f32[18,1,128,128]{3,2,1,0:T(8,128)S(1)}, f32[18,1,128,128]{3,2,1,0:T(8,128)S(1)}, u32[]{:S(2)}, u32[]{:S(2)}) %collective-permute-start.14) | collective-permute-done | bytes 1179680 | tf_op jit(solution)/shard_map/ppermute | solution.py:16
  213.8 30.9 %fusion.27 = f32[16,8,128,128]{3,2,1,0:T(8,128)} fusion(f32[16,8,128,128]{3,2,1,0:T(8,128)} %param.7, f32[18,10,1,128]{3,2,1,0:T(1,128)S(1)} %copy.37, f32[18,1,128,128]{3,2,1,0:T(8,128)S(1)} %collective-permute-done.15, f32[18,1,128,128]{3,2,1,0:T(8,128)S(1)} %collective-permute-done.14, f32[1,8,128,128]{3,2,1,0:T(8,128)S(1)} %collective-permute-done.13, ...), kind=kLoop, calls=%fused_computation.83 | loop fusion | flops 60817408 | bytes 37146624 | tf_op jit(solution)/shard_map/add | solution.py:51
  246.1 7.5 %collective-permute-start.18 = (f32[1,8,128,128]{3,2,1,0:T(8,128)S(1)}, f32[1,8,128,128]{3,2,1,0:T(8,128)S(1)}, u32[]{:S(2)}, u32[]{:S(2)}) collective-permute-start(f32[1,8,128,128]{3,2,1,0:T(8,128)S(1)} %get-tuple-element.147), channel_id=1, source_target_pairs={{0,8},{8,16},{16,24},{1,9},{9,17},{17,25},{2,10},{10,18},{18,26},{... | collective-permute-start | bytes 1572872 | tf_op jit(solution)/shard_map/ppermute | solution.py:16
  260.8 5.1 collective-permute-start.21
  265.9 18.0 %collective-permute-done.20 = f32[18,1,128,128]{3,2,1,0:T(8,128)S(1)} collective-permute-done((f32[18,1,128,128]{3,2,1,0:T(8,128)S(1)}, f32[18,1,128,128]{3,2,1,0:T(8,128)S(1)}, u32[]{:S(2)}, u32[]{:S(2)}) %collective-permute-start.20) | collective-permute-done | bytes 1179680 | tf_op jit(solution)/shard_map/ppermute | solution.py:16
  294.2 31.0 %fusion.19 = f32[16,8,128,128]{3,2,1,0:T(8,128)} fusion(f32[16,8,128,128]{3,2,1,0:T(8,128)} %param.7, f32[18,10,1,128]{3,2,1,0:T(1,128)S(1)} %copy.41, f32[18,1,128,128]{3,2,1,0:T(8,128)S(1)} %collective-permute-done.21, f32[18,1,128,128]{3,2,1,0:T(8,128)S(1)} %collective-permute-done.20, f32[1,8,128,128]{3,2,1,0:T(8,128)S(1)} %collective-permute-done.19, ...), kind=kLoop, calls=%fused_computation.57 | loop fusion | flops 60817408 | bytes 37146624 | tf_op jit(solution)/shard_map/add | solution.py:51
  326.7 7.5 %collective-permute-start.24 = (f32[1,8,128,128]{3,2,1,0:T(8,128)S(1)}, f32[1,8,128,128]{3,2,1,0:T(8,128)S(1)}, u32[]{:S(2)}, u32[]{:S(2)}) collective-permute-start(f32[1,8,128,128]{3,2,1,0:T(8,128)S(1)} %get-tuple-element.145), channel_id=1, source_target_pairs={{0,8},{8,16},{16,24},{1,9},{9,17},{17,25},{2,10},{10,18},{18,26},{... | collective-permute-start | bytes 1572872 | tf_op jit(solution)/shard_map/ppermute | solution.py:16
  341.4 5.1 collective-permute-start.27
  346.5 18.0 %collective-permute-done.26 = f32[18,1,128,128]{3,2,1,0:T(8,128)S(1)} collective-permute-done((f32[18,1,128,128]{3,2,1,0:T(8,128)S(1)}, f32[18,1,128,128]{3,2,1,0:T(8,128)S(1)}, u32[]{:S(2)}, u32[]{:S(2)}) %collective-permute-start.26) | collective-permute-done | bytes 1179680 | tf_op jit(solution)/shard_map/ppermute | solution.py:16
  374.8 30.9 %fusion.11 = f32[16,8,128,128]{3,2,1,0:T(8,128)} fusion(f32[16,8,128,128]{3,2,1,0:T(8,128)} %param.7, f32[18,10,1,128]{3,2,1,0:T(1,128)S(1)} %copy.45, f32[18,1,128,128]{3,2,1,0:T(8,128)S(1)} %collective-permute-done.27, f32[18,1,128,128]{3,2,1,0:T(8,128)S(1)} %collective-permute-done.26, f32[1,8,128,128]{3,2,1,0:T(8,128)S(1)} %collective-permute-done.25, ...), kind=kLoop, calls=%fused_computation.31 | loop fusion | flops 60817408 | bytes 37146624 | tf_op jit(solution)/shard_map/add | solution.py:51
  407.2 7.5 %collective-permute-start.30 = (f32[1,8,128,128]{3,2,1,0:T(8,128)S(1)}, f32[1,8,128,128]{3,2,1,0:T(8,128)S(1)}, u32[]{:S(2)}, u32[]{:S(2)}) collective-permute-start(f32[1,8,128,128]{3,2,1,0:T(8,128)S(1)} %get-tuple-element.143), channel_id=1, source_target_pairs={{0,8},{8,16},{16,24},{1,9},{9,17},{17,25},{2,10},{10,18},{18,26},{... | collective-permute-start | bytes 1572872 | tf_op jit(solution)/shard_map/ppermute | solution.py:16
  426.9 18.0 %collective-permute-done.32 = f32[18,1,128,128]{3,2,1,0:T(8,128)S(1)} collective-permute-done((f32[18,1,128,128]{3,2,1,0:T(8,128)S(1)}, f32[18,1,128,128]{3,2,1,0:T(8,128)S(1)}, u32[]{:S(2)}, u32[]{:S(2)}) %collective-permute-start.32) | collective-permute-done | bytes 1179680 | tf_op jit(solution)/shard_map/ppermute | solution.py:16
  455.3 31.0 %fusion.3 = f32[16,8,128,128]{3,2,1,0:T(8,128)} fusion(f32[16,8,128,128]{3,2,1,0:T(8,128)} %param.7, f32[18,10,1,128]{3,2,1,0:T(1,128)S(1)} %copy.49, f32[18,1,128,128]{3,2,1,0:T(8,128)S(1)} %collective-permute-done.33, f32[18,1,128,128]{3,2,1,0:T(8,128)S(1)} %collective-permute-done.32, f32[1,8,128,128]{3,2,1,0:T(8,128)S(1)} %collective-permute-done.31, ...), kind=kLoop, calls=%fused_computation.5 | loop fusion | flops 60817408 | bytes 37146624 | tf_op jit(solution)/shard_map/add | solution.py:51
  486.3 8.4 %fusion.55 = f32[16,8,128,128]{3,2,1,0:T(8,128)} fusion(f32[16,8,128,128]{3,2,1,0:T(8,128)} %fusion.3), kind=kOutput, calls=%fused_computation.203 | output fusion | flops 14680064 | bytes 16777216 | tf_op jit(solution)/shard_map/jit(cumsum)/reduce_window_sum | solution.py:59
  497.0 84.4 %all-gather.3.cloned.1.call-done = f32[64,1,128,128]{3,2,1,0:T(8,128)} async-done(((f32[16,1,128,128]{3,2,1,0:T(8,128)}), f32[64,1,128,128]{3,2,1,0:T(8,128)}) %all-gather.3.cloned.1.call-update) | async-done | bytes 4194320 | tf_op jit(solution)/shard_map/all_gather | solution.py:24
  586.2 8.7 %add_multiply_fusion = f32[16,8,128,128]{3,2,1,0:T(8,128)} fusion(f32[16,8,128,128]{3,2,1,0:T(8,128)} %fusion.55, f32[16,128,128]{2,1,0:T(8,128)S(1)} %bitcast.11), kind=kLoop, calls=%fused_computation.149 | loop fusion | flops 4194304 | bytes 17825792 | tf_op jit(solution)/shard_map/div | solution.py:66
  (133 shorter events, 142.0 us)
Async XLA Ops:
  7.2 574.2 %all-gather.3.cloned.1.call-start = ((), (), s32[]{:S(2)}) async-start(), calls=%async_computation | async-start | bytes 5242880 | tf_op jit(solution)/shard_map/all_gather | solution.py:24
  16.9 25.7 %collective-permute-start.2 = (f32[18,1,128,128]{3,2,1,0:T(8,128)S(1)}, f32[18,1,128,128]{3,2,1,0:T(8,128)S(1)}, u32[]{:S(2)}, u32[]{:S(2)}) collective-permute-start(f32[18,1,128,128]{3,2,1,0:T(8,128)S(1)} %get-tuple-element.141), channel_id=1, source_target_pairs={{0,2},{2,4},{4,6},{1,3},{3,5},{5,7},{8,10},{10,12},{12,14},{9,11},... | collective-permute-start | bytes 3538952 | tf_op jit(solution)/shard_map/ppermute | solution.py:16
  18.5 26.0 %collective-permute-start.3 = (f32[18,1,128,128]{3,2,1,0:T(8,128)S(1)}, f32[18,1,128,128]{3,2,1,0:T(8,128)S(1)}, u32[]{:S(2)}, u32[]{:S(2)}) collective-permute-start(f32[18,1,128,128]{3,2,1,0:T(8,128)S(1)} %get-tuple-element.142), channel_id=1, source_target_pairs={{2,0},{4,2},{6,4},{3,1},{5,3},{7,5},{10,8},{12,10},{14,12},{11,9},... | collective-permute-start | bytes 3538952 | tf_op jit(solution)/shard_map/ppermute | solution.py:17
  48.2 6.8 %collective-permute-start.5 = (f32[18,10,1,128]{3,0,2,1:T(8,128)S(1)}, f32[18,10,1,128]{3,0,2,1:T(8,128)S(1)}, u32[]{:S(2)}, u32[]{:S(2)}) collective-permute-start(f32[18,10,1,128]{3,0,2,1:T(8,128)S(1)} %copy.28), channel_id=1, source_target_pairs={{1,0},{3,2},{5,4},{7,6},{9,8},{11,10},{13,12},{15,14},{17,16},{19,... | collective-permute-start | bytes 276488 | tf_op jit(solution)/shard_map/ppermute | solution.py:17
  84.8 7.6 %collective-permute-start.6 = (f32[1,8,128,128]{3,2,1,0:T(8,128)S(1)}, f32[1,8,128,128]{3,2,1,0:T(8,128)S(1)}, u32[]{:S(2)}, u32[]{:S(2)}) collective-permute-start(f32[1,8,128,128]{3,2,1,0:T(8,128)S(1)} %get-tuple-element.151), channel_id=1, source_target_pairs={{0,8},{8,16},{16,24},{1,9},{9,17},{17,25},{2,10},{10,18},{18,26},{... | collective-permute-start | bytes 1572872 | tf_op jit(solution)/shard_map/ppermute | solution.py:16
  98.8 24.4 %collective-permute-start.8 = (f32[18,1,128,128]{3,2,1,0:T(8,128)S(1)}, f32[18,1,128,128]{3,2,1,0:T(8,128)S(1)}, u32[]{:S(2)}, u32[]{:S(2)}) collective-permute-start(f32[18,1,128,128]{3,2,1,0:T(8,128)S(1)} %get-tuple-element.139), channel_id=1, source_target_pairs={{0,2},{2,4},{4,6},{1,3},{3,5},{5,7},{8,10},{10,12},{12,14},{9,11},... | collective-permute-start | bytes 3538952 | tf_op jit(solution)/shard_map/ppermute | solution.py:16
  100.1 24.8 %collective-permute-start.9 = (f32[18,1,128,128]{3,2,1,0:T(8,128)S(1)}, f32[18,1,128,128]{3,2,1,0:T(8,128)S(1)}, u32[]{:S(2)}, u32[]{:S(2)}) collective-permute-start(f32[18,1,128,128]{3,2,1,0:T(8,128)S(1)} %get-tuple-element.140), channel_id=1, source_target_pairs={{2,0},{4,2},{6,4},{3,1},{5,3},{7,5},{10,8},{12,10},{14,12},{11,9},... | collective-permute-start | bytes 3538952 | tf_op jit(solution)/shard_map/ppermute | solution.py:17
  126.6 6.8 %collective-permute-start.11 = (f32[18,10,1,128]{3,0,2,1:T(8,128)S(1)}, f32[18,10,1,128]{3,0,2,1:T(8,128)S(1)}, u32[]{:S(2)}, u32[]{:S(2)}) collective-permute-start(f32[18,10,1,128]{3,0,2,1:T(8,128)S(1)} %copy.32), channel_id=1, source_target_pairs={{1,0},{3,2},{5,4},{7,6},{9,8},{11,10},{13,12},{15,14},{17,16},{19,... | collective-permute-start | bytes 276488 | tf_op jit(solution)/shard_map/ppermute | solution.py:17
  165.7 9.0 %collective-permute-start.12 = (f32[1,8,128,128]{3,2,1,0:T(8,128)S(1)}, f32[1,8,128,128]{3,2,1,0:T(8,128)S(1)}, u32[]{:S(2)}, u32[]{:S(2)}) collective-permute-start(f32[1,8,128,128]{3,2,1,0:T(8,128)S(1)} %get-tuple-element.149), channel_id=1, source_target_pairs={{0,8},{8,16},{16,24},{1,9},{9,17},{17,25},{2,10},{10,18},{18,26},{... | collective-permute-start | bytes 1572872 | tf_op jit(solution)/shard_map/ppermute | solution.py:16
  179.1 24.4 %collective-permute-start.14 = (f32[18,1,128,128]{3,2,1,0:T(8,128)S(1)}, f32[18,1,128,128]{3,2,1,0:T(8,128)S(1)}, u32[]{:S(2)}, u32[]{:S(2)}) collective-permute-start(f32[18,1,128,128]{3,2,1,0:T(8,128)S(1)} %get-tuple-element.137), channel_id=1, source_target_pairs={{0,2},{2,4},{4,6},{1,3},{3,5},{5,7},{8,10},{10,12},{12,14},{9,11},... | collective-permute-start | bytes 3538952 | tf_op jit(solution)/shard_map/ppermute | solution.py:16
  180.4 24.8 %collective-permute-start.15 = (f32[18,1,128,128]{3,2,1,0:T(8,128)S(1)}, f32[18,1,128,128]{3,2,1,0:T(8,128)S(1)}, u32[]{:S(2)}, u32[]{:S(2)}) collective-permute-start(f32[18,1,128,128]{3,2,1,0:T(8,128)S(1)} %get-tuple-element.138), channel_id=1, source_target_pairs={{2,0},{4,2},{6,4},{3,1},{5,3},{7,5},{10,8},{12,10},{14,12},{11,9},... | collective-permute-start | bytes 3538952 | tf_op jit(solution)/shard_map/ppermute | solution.py:17
  206.9 6.8 %collective-permute-start.17 = (f32[18,10,1,128]{3,0,2,1:T(8,128)S(1)}, f32[18,10,1,128]{3,0,2,1:T(8,128)S(1)}, u32[]{:S(2)}, u32[]{:S(2)}) collective-permute-start(f32[18,10,1,128]{3,0,2,1:T(8,128)S(1)} %copy.36), channel_id=1, source_target_pairs={{1,0},{3,2},{5,4},{7,6},{9,8},{11,10},{13,12},{15,14},{17,16},{19,... | collective-permute-start | bytes 276488 | tf_op jit(solution)/shard_map/ppermute | solution.py:17
  246.1 9.3 %collective-permute-start.18 = (f32[1,8,128,128]{3,2,1,0:T(8,128)S(1)}, f32[1,8,128,128]{3,2,1,0:T(8,128)S(1)}, u32[]{:S(2)}, u32[]{:S(2)}) collective-permute-start(f32[1,8,128,128]{3,2,1,0:T(8,128)S(1)} %get-tuple-element.147), channel_id=1, source_target_pairs={{0,8},{8,16},{16,24},{1,9},{9,17},{17,25},{2,10},{10,18},{18,26},{... | collective-permute-start | bytes 1572872 | tf_op jit(solution)/shard_map/ppermute | solution.py:16
  259.5 24.4 %collective-permute-start.20 = (f32[18,1,128,128]{3,2,1,0:T(8,128)S(1)}, f32[18,1,128,128]{3,2,1,0:T(8,128)S(1)}, u32[]{:S(2)}, u32[]{:S(2)}) collective-permute-start(f32[18,1,128,128]{3,2,1,0:T(8,128)S(1)} %get-tuple-element.135), channel_id=1, source_target_pairs={{0,2},{2,4},{4,6},{1,3},{3,5},{5,7},{8,10},{10,12},{12,14},{9,11},... | collective-permute-start | bytes 3538952 | tf_op jit(solution)/shard_map/ppermute | solution.py:16
  260.8 24.8 %collective-permute-start.21 = (f32[18,1,128,128]{3,2,1,0:T(8,128)S(1)}, f32[18,1,128,128]{3,2,1,0:T(8,128)S(1)}, u32[]{:S(2)}, u32[]{:S(2)}) collective-permute-start(f32[18,1,128,128]{3,2,1,0:T(8,128)S(1)} %get-tuple-element.136), channel_id=1, source_target_pairs={{2,0},{4,2},{6,4},{3,1},{5,3},{7,5},{10,8},{12,10},{14,12},{11,9},... | collective-permute-start | bytes 3538952 | tf_op jit(solution)/shard_map/ppermute | solution.py:17
  287.3 6.8 %collective-permute-start.23 = (f32[18,10,1,128]{3,0,2,1:T(8,128)S(1)}, f32[18,10,1,128]{3,0,2,1:T(8,128)S(1)}, u32[]{:S(2)}, u32[]{:S(2)}) collective-permute-start(f32[18,10,1,128]{3,0,2,1:T(8,128)S(1)} %copy.40), channel_id=1, source_target_pairs={{1,0},{3,2},{5,4},{7,6},{9,8},{11,10},{13,12},{15,14},{17,16},{19,... | collective-permute-start | bytes 276488 | tf_op jit(solution)/shard_map/ppermute | solution.py:17
  326.7 9.0 %collective-permute-start.24 = (f32[1,8,128,128]{3,2,1,0:T(8,128)S(1)}, f32[1,8,128,128]{3,2,1,0:T(8,128)S(1)}, u32[]{:S(2)}, u32[]{:S(2)}) collective-permute-start(f32[1,8,128,128]{3,2,1,0:T(8,128)S(1)} %get-tuple-element.145), channel_id=1, source_target_pairs={{0,8},{8,16},{16,24},{1,9},{9,17},{17,25},{2,10},{10,18},{18,26},{... | collective-permute-start | bytes 1572872 | tf_op jit(solution)/shard_map/ppermute | solution.py:16
  340.1 24.4 %collective-permute-start.26 = (f32[18,1,128,128]{3,2,1,0:T(8,128)S(1)}, f32[18,1,128,128]{3,2,1,0:T(8,128)S(1)}, u32[]{:S(2)}, u32[]{:S(2)}) collective-permute-start(f32[18,1,128,128]{3,2,1,0:T(8,128)S(1)} %get-tuple-element.133), channel_id=1, source_target_pairs={{0,2},{2,4},{4,6},{1,3},{3,5},{5,7},{8,10},{10,12},{12,14},{9,11},... | collective-permute-start | bytes 3538952 | tf_op jit(solution)/shard_map/ppermute | solution.py:16
  341.4 24.8 %collective-permute-start.27 = (f32[18,1,128,128]{3,2,1,0:T(8,128)S(1)}, f32[18,1,128,128]{3,2,1,0:T(8,128)S(1)}, u32[]{:S(2)}, u32[]{:S(2)}) collective-permute-start(f32[18,1,128,128]{3,2,1,0:T(8,128)S(1)} %get-tuple-element.134), channel_id=1, source_target_pairs={{2,0},{4,2},{6,4},{3,1},{5,3},{7,5},{10,8},{12,10},{14,12},{11,9},... | collective-permute-start | bytes 3538952 | tf_op jit(solution)/shard_map/ppermute | solution.py:17
  367.9 6.8 %collective-permute-start.29 = (f32[18,10,1,128]{3,0,2,1:T(8,128)S(1)}, f32[18,10,1,128]{3,0,2,1:T(8,128)S(1)}, u32[]{:S(2)}, u32[]{:S(2)}) collective-permute-start(f32[18,10,1,128]{3,0,2,1:T(8,128)S(1)} %copy.44), channel_id=1, source_target_pairs={{1,0},{3,2},{5,4},{7,6},{9,8},{11,10},{13,12},{15,14},{17,16},{19,... | collective-permute-start | bytes 276488 | tf_op jit(solution)/shard_map/ppermute | solution.py:17
  407.2 9.0 %collective-permute-start.30 = (f32[1,8,128,128]{3,2,1,0:T(8,128)S(1)}, f32[1,8,128,128]{3,2,1,0:T(8,128)S(1)}, u32[]{:S(2)}, u32[]{:S(2)}) collective-permute-start(f32[1,8,128,128]{3,2,1,0:T(8,128)S(1)} %get-tuple-element.143), channel_id=1, source_target_pairs={{0,8},{8,16},{16,24},{1,9},{9,17},{17,25},{2,10},{10,18},{18,26},{... | collective-permute-start | bytes 1572872 | tf_op jit(solution)/shard_map/ppermute | solution.py:16
  420.6 24.4 %collective-permute-start.32 = (f32[18,1,128,128]{3,2,1,0:T(8,128)S(1)}, f32[18,1,128,128]{3,2,1,0:T(8,128)S(1)}, u32[]{:S(2)}, u32[]{:S(2)}) collective-permute-start(f32[18,1,128,128]{3,2,1,0:T(8,128)S(1)} %get-tuple-element.131), channel_id=1, source_target_pairs={{0,2},{2,4},{4,6},{1,3},{3,5},{5,7},{8,10},{10,12},{12,14},{9,11},... | collective-permute-start | bytes 3538952 | tf_op jit(solution)/shard_map/ppermute | solution.py:16
  421.9 24.8 %collective-permute-start.33 = (f32[18,1,128,128]{3,2,1,0:T(8,128)S(1)}, f32[18,1,128,128]{3,2,1,0:T(8,128)S(1)}, u32[]{:S(2)}, u32[]{:S(2)}) collective-permute-start(f32[18,1,128,128]{3,2,1,0:T(8,128)S(1)} %get-tuple-element.132), channel_id=1, source_target_pairs={{2,0},{4,2},{6,4},{3,1},{5,3},{7,5},{10,8},{12,10},{14,12},{11,9},... | collective-permute-start | bytes 3538952 | tf_op jit(solution)/shard_map/ppermute | solution.py:17
  448.4 6.8 %collective-permute-start.35 = (f32[18,10,1,128]{3,0,2,1:T(8,128)S(1)}, f32[18,10,1,128]{3,0,2,1:T(8,128)S(1)}, u32[]{:S(2)}, u32[]{:S(2)}) collective-permute-start(f32[18,10,1,128]{3,0,2,1:T(8,128)S(1)} %copy.48), channel_id=1, source_target_pairs={{1,0},{3,2},{5,4},{7,6},{9,8},{11,10},{13,12},{15,14},{17,16},{19,... | collective-permute-start | bytes 276488 | tf_op jit(solution)/shard_map/ppermute | solution.py:17
  (24 other events, 373.0 us)
Sparse Core Ops, SparseCore 0:
  497.1 84.2 all-gather.2
where the time goes:
time: 613 us; the launch traced here: 602 us
  waiting for transfers between devices  252 us (41%)
  other arithmetic  214 us (35%)
  starting transfers between devices  104 us (17%)
  local copies, waits for them, and re-layouts  17.2 us (3%)
  between operations  14.9 us (2%)
    add x6, other arithmetic, advance(): return 2.0 * middle - before + speed_square * spread  183 us
    ppermute x18, waiting for transfers between devices, padded_2(): before = lax.ppermute(last, axis, up)  116 us
    all_gather x1, waiting for transfers between devices, prefix(): pieces = lax.all_gather(value, axis)  84.4 us
    ppermute x18, starting transfers between devices, padded_2(): before = lax.ppermute(last, axis, up)  56.8 us
    ppermute x18, waiting for transfers between devices, padded_2(): after = lax.ppermute(initial, axis, down)  51.5 us
    ppermute x18, starting transfers between devices, padded_2(): after = lax.ppermute(initial, axis, down)  47.2 us
  transfers between devices with their start and end apart: 37, of which 35 were waited for; matrix products, arithmetic and copies ran while one was open for 1% of the time, Pallas kernels for 0%

commit v1 on v0

v1 whole, which is shorter than its diff:
```python
import functools

import jax
import jax.numpy as jnp
from jax import lax
from jax.experimental import pallas as pl
from jax.experimental.pallas import tpu as pltpu
from jax.sharding import PartitionSpec as P

STEPS = 6
PAD = 8
MESH = pl.DeviceIdType.MESH
AXES = ("rows", "cols", "slabs")


def kernel(counts, block, p_hbm, e_hbm, c_hbm, sum_hbm, end_hbm, field, speed, z_out, z_in, sum_in, sum_out,
           load_sem, x_send, x_recv, y_send, y_recv, z_send, z_recv, s_send, s_recv, store_sem):
    ny, nx, nz, _ = block
    chunk = 32 if nz % 32 == 0 else 8
    me = [lax.axis_index(axis) for axis in AXES]
    has = [(me[d] > 0, me[d] < counts[d] - 1) for d in range(3)]

    def other(d, side):
        return {AXES[d]: me[d] + (1 if side else -1)}

    def each(d):
        for side in (0, 1):
            if counts[d] > 1:
                yield side, has[d][side]

    core_z = pl.ds(PAD, nz)

    def load(which, y):
        hbm = (p_hbm, e_hbm, c_hbm)[which]
        dst = speed.at[y] if which == 2 else field.at[which, y + 1, pl.ds(1, nx), core_z, :]
        return pltpu.make_async_copy(hbm.at[y], dst, load_sem.at[which, y])

    def order(i):
        return (i + ny - 1) % ny

    def loads(i, _, which):
        for w in which:
            load(w, order(i)).start()
        return 0

    lax.fori_loop(0, ny, functools.partial(loads, which=(0,)), 0)
    lax.fori_loop(0, ny, functools.partial(loads, which=(1, 2)), 0)

    def x_copy(par, y, side, first=False):
        cell = nx - 1 if side else 0
        src = p_hbm.at[y, cell] if first else field.at[par, y + 1, cell + 1, core_z, :]
        return pltpu.make_async_remote_copy(
            src_ref=src,
            dst_ref=field.at[par, y + 1, 0 if side else nx + 1, core_z, :],
            send_sem=x_send.at[par, side, y], recv_sem=x_recv.at[par, 1 - side, y],
            device_id=other(1, side), device_id_type=MESH)

    def x_wait(par, y, side):
        here = field.at[par, y + 1, nx + 1 if side else 0, core_z, :]
        return pltpu.make_async_remote_copy(
            src_ref=here, dst_ref=here,
            send_sem=x_send.at[par, side, y], recv_sem=x_recv.at[par, side, y],
            device_id=other(1, side), device_id_type=MESH)

    def y_copy(par, side, first=False):
        cell = ny - 1 if side else 0
        src = p_hbm.at[cell] if first else field.at[par, cell + 1, pl.ds(1, nx), core_z, :]
        return pltpu.make_async_remote_copy(
            src_ref=src,
            dst_ref=field.at[par, 0 if side else ny + 1, pl.ds(1, nx), core_z, :],
            send_sem=y_send.at[par, side], recv_sem=y_recv.at[par, 1 - side],
            device_id=other(0, side), device_id_type=MESH)

    def y_wait(par, side):
        here = field.at[par, ny + 1 if side else 0, pl.ds(1, nx), core_z, :]
        return pltpu.make_async_remote_copy(
            src_ref=here, dst_ref=here,
            send_sem=y_send.at[par, side], recv_sem=y_recv.at[par, side],
            device_id=other(0, side), device_id_type=MESH)

    def z_copy(par, y, side):
        return pltpu.make_async_remote_copy(
            src_ref=z_out.at[par, side, y], dst_ref=z_in.at[par, 1 - side, y],
            send_sem=z_send.at[par, side, y], recv_sem=z_recv.at[par, 1 - side, y],
            device_id=other(2, side), device_id_type=MESH)

    def z_wait(par, y, side):
        here = z_in.at[par, side, y]
        return pltpu.make_async_remote_copy(
            src_ref=here, dst_ref=here,
            send_sem=z_send.at[par, side, y], recv_sem=z_recv.at[par, side, y],
            device_id=other(2, side), device_id_type=MESH)

    def s_copy(y):
        return pltpu.make_async_remote_copy(
            src_ref=sum_out.at[y], dst_ref=sum_in.at[y],
            send_sem=s_send.at[y], recv_sem=s_recv.at[y],
            device_id=other(1, 1), device_id_type=MESH)

    def s_wait(y):
        return pltpu.make_async_remote_copy(
            src_ref=sum_in.at[y], dst_ref=sum_in.at[y],
            send_sem=s_send.at[y], recv_sem=s_recv.at[y],
            device_id=other(1, 0), device_id_type=MESH)

    barrier = pltpu.get_barrier_semaphore()
    for d in range(3):
        for side, there in each(d):
            @pl.when(there)
            def _():
                pl.semaphore_signal(barrier, inc=1, device_id=other(d, side), device_id_type=MESH)
    peers = sum(there.astype(jnp.int32) for d in range(3) for _, there in each(d))
    pl.semaphore_wait(barrier, peers)

    for side, there in each(0):
        @pl.when(there)
        def _():
            y_copy(0, side, True).start()
    def first_x(i, _):
        for side, there in each(1):
            @pl.when(there)
            def _():
                x_copy(0, order(i), side, True).start()
        return 0
    lax.fori_loop(0, ny, first_x, 0)

    lanes = block[3]
    def zero_x(side):
        def body(y, _):
            for par in (0, 1):
                field[par, y + 1, nx + 1 if side else 0, core_z, :] = jnp.zeros((nz, lanes), jnp.float32)
            return 0
        lax.fori_loop(0, ny, body, 0)
    def zero_y(side):
        def body(x, _):
            for par in (0, 1):
                field[par, ny + 1 if side else 0, x + 1, core_z, :] = jnp.zeros((nz, lanes), jnp.float32)
            return 0
        lax.fori_loop(0, nx, body, 0)
    def zero_z(side):
        def body(y, _):
            for par in (0, 1):
                for x in range(nx):
                    field[par, y + 1, x + 1, pl.ds(PAD + nz if side else 0, PAD), :] = jnp.zeros((PAD, lanes), jnp.float32)
            return 0
        lax.fori_loop(0, ny, body, 0)
    def zero_s(y, _):
        sum_in[y] = jnp.zeros((nz, lanes), jnp.float32)
        return 0
    for d, zero in ((0, zero_y), (1, zero_x), (2, zero_z)):
        for side in (0, 1):
            pl.when(jnp.logical_not(has[d][side]))(functools.partial(zero, side))
    @pl.when(jnp.logical_not(has[1][0]))
    def _():
        lax.fori_loop(0, ny, zero_s, 0)

    def send_z(par, y):
        for side, there in each(2):
            @pl.when(there)
            def _():
                row = PAD + nz - 1 if side else PAD
                for x in range(nx):
                    z_out[par, side, y, pl.ds(x, 1), :] = field[par, y + 1, x + 1, pl.ds(row, 1), :]
                z_copy(par, y, side).start()

    def first_z(i, _):
        y = order(i)
        load(0, y).wait()
        send_z(0, y)
        return 0
    lax.fori_loop(0, ny, first_z, 0)

    def arrive(par, y):
        for side, there in each(1):
            @pl.when(there)
            def _():
                x_wait(par, y, side).wait_recv()
        for side, there in each(0):
            @pl.when(jnp.logical_and(there, y == (ny - 1 if side else 0)))
            def _():
                y_wait(par, side).wait_recv()
        for side, there in each(2):
            @pl.when(there)
            def _():
                z_wait(par, y, side).wait_recv()
                row = PAD + nz if side else PAD - 1
                for x in range(nx):
                    field[par, y + 1, x + 1, pl.ds(row, 1), :] = z_in[par, side, y, pl.ds(x, 1), :]

    def sent(par, y):
        for side, there in each(1):
            @pl.when(there)
            def _():
                x_copy(par, y, side).wait_send()
        for side, there in each(0):
            @pl.when(jnp.logical_and(there, y == (ny - 1 if side else 0)))
            def _():
                y_copy(par, side).wait_send()
        for side, there in each(2):
            @pl.when(there)
            def _():
                z_copy(par, y, side).wait_send()

    def cell(par, y, x, z):
        def at(dy, dx, dz):
            return field[par, y + 1 + dy, x + 1 + dx, pl.ds(PAD + z + dz, chunk), :]
        middle = at(0, 0, 0)
        spread = (at(-1, 0, 0) + at(1, 0, 0) + at(0, -1, 0) + at(0, 1, 0) + at(0, 0, -1) + at(0, 0, 1)
                  - 6.0 * middle)
        before = field[1 - par, y + 1, x + 1, pl.ds(PAD + z, chunk), :]
        later = 2.0 * middle - before + speed[y, x, pl.ds(z, chunk), :] * spread
        field[1 - par, y + 1, x + 1, pl.ds(PAD + z, chunk), :] = later
        return later

    def step(t, _):
        par = t % 2
        def row(i, _):
            y = order(i)
            @pl.when(t == 0)
            def _():
                load(1, y).wait()
                load(2, y).wait()
            arrive(par, y)
            @pl.when(t > 0)
            def _():
                sent(1 - par, y)
            def along(x, _):
                for z in range(0, nz, chunk):
                    cell(par, y, x, z)
                return 0
            lax.fori_loop(0, nx, along, 0)
            for side, there in each(1):
                @pl.when(there)
                def _():
                    x_copy(1 - par, y, side).start()
            for side, there in each(0):
                @pl.when(jnp.logical_and(there, y == (ny - 1 if side else 0)))
                def _():
                    y_copy(1 - par, side).start()
            send_z(1 - par, y)
            return 0
        lax.fori_loop(0, ny, row, 0)
        return 0
    lax.fori_loop(0, STEPS - 1, step, 0)

    last = (STEPS - 1) % 2

    def end_copy(y):
        return pltpu.make_async_copy(field.at[1 - last, y + 1, pl.ds(1, nx), core_z, :], end_hbm.at[y], store_sem.at[0, y])

    def sum_copy(y):
        return pltpu.make_async_copy(speed.at[y], sum_hbm.at[y], store_sem.at[1, y])

    def last_row(i, _):
        y = order(i)
        arrive(last, y)
        sent(1 - last, y)
        for z in range(0, nz, chunk):
            def along(x, total):
                total = total + cell(last, y, x, z)
                speed[y, x, pl.ds(z, chunk), :] = total
                return total
            total = lax.fori_loop(0, nx, along, jnp.zeros((chunk, lanes), jnp.float32))
            @pl.when(jnp.logical_not(has[1][0]))
            def _():
                sum_out[y, pl.ds(z, chunk), :] = total
        if counts[1] > 1:
            @pl.when(jnp.logical_not(has[1][0]))
            def _():
                s_copy(y).start()
        end_copy(y).start()
        return 0
    lax.fori_loop(0, ny, last_row, 0)

    scale = 1.0 / (nx * counts[1])

    def finish(i, _):
        y = order(i)
        if counts[1] > 1:
            @pl.when(has[1][0])
            def _():
                s_wait(y).wait_recv()
                @pl.when(has[1][1])
                def _():
                    for z in range(0, nz, chunk):
                        at = pl.ds(z, chunk)
                        sum_out[y, at, :] = sum_in[y, at, :] + speed[y, nx - 1, at, :]
                    s_copy(y).start()
        for z in range(0, nz, chunk):
            at = pl.ds(z, chunk)
            below = sum_in[y, at, :]
            def along(x, _):
                speed[y, x, at, :] = (speed[y, x, at, :] + below) * scale
                return 0
            lax.fori_loop(0, nx, along, 0)
        sum_copy(y).start()
        return 0
    lax.fori_loop(0, ny, finish, 0)

    def drain(i, _):
        y = order(i)
        sent(last, y)
        if counts[1] > 1:
            @pl.when(has[1][1])
            def _():
                s_copy(y).wait_send()
        end_copy(y).wait()
        sum_copy(y).wait()
        return 0
    lax.fori_loop(0, ny, drain, 0)


def solution(mesh):
    counts = tuple(mesh.shape[axis] for axis in AXES)

    def on_device(pressure, earlier, speed_square):
        block = pressure.shape
        ny, nx, nz, lanes = block
        f32 = jnp.float32
        anywhere = pl.BlockSpec(memory_space=pl.ANY)
        dma = pltpu.SemaphoreType.DMA
        return pl.pallas_call(
            functools.partial(kernel, counts, block),
            out_shape=[jax.ShapeDtypeStruct(block, f32)] * 2,
            in_specs=[anywhere] * 3,
            out_specs=[anywhere] * 2,
            scratch_shapes=[
                pltpu.VMEM((2, ny + 2, nx + 2, nz + 2 * PAD, lanes), f32),
                pltpu.VMEM((ny, nx, nz, lanes), f32),
                pltpu.VMEM((2, 2, ny, nx, lanes), f32),
                pltpu.VMEM((2, 2, ny, nx, lanes), f32),
                pltpu.VMEM((ny, nz, lanes), f32),
                pltpu.VMEM((ny, nz, lanes), f32),
                dma((3, ny)),
                dma((2, 2, ny)), dma((2, 2, ny)),
                dma((2, 2)), dma((2, 2)),
                dma((2, 2, ny)), dma((2, 2, ny)),
                dma((ny,)), dma((ny,)),
                dma((2, ny)),
            ],
            compiler_params=pltpu.CompilerParams(
                collective_id=0, has_side_effects=True, vmem_limit_bytes=60 * 1024 * 1024
            ),
        )(pressure, earlier, speed_square)

    spec = P("rows", "cols", "slabs", None)
    return jax.shard_map(
        on_device, mesh=mesh, in_specs=(spec, spec, spec), out_specs=(spec, spec), check_vma=False
    )
```

time: 613 us -> 183 us (0.30); the launches traced: 602 us -> 183 us
  waiting for transfers between devices: 252 us -> 0 us
  other arithmetic: 214 us -> 0 us
  Pallas kernels: 0 us -> 171 us
  starting transfers between devices: 104 us -> 0 us
  between operations: 14.9 us -> 0.65 us
    add x6 -> x0, other arithmetic: 183 us -> none  [advance(): return 2.0 * middle - before + speed_square * spread]
    pallas_call x0 -> x1, Pallas kernels: none -> 171 us  [on_device(): pl.pallas_call(functools.partial(kernel, counts, block), out_shape=[jax.S...]
    ppermute x36 -> x0, waiting for transfers between devices: 167 us -> none  [the longest x18 116 us: padded_2(): before = lax.ppermute(last, axis, up)]
    ppermute x36 -> x0, starting transfers between devices: 104 us -> none  [the longest x18 56.8 us: padded_2(): before = lax.ppermute(last, axis, up)]
    all_gather x1 -> x0, waiting for transfers between devices: 84.4 us -> none  [prefix(): pieces = lax.all_gather(value, axis)]
    slice x20 -> x0, local copies, waits for them, and re-layouts: 11.2 us -> none  [the longest x12 7.53 us: padded_2(): last = lax.slice_in_dim(x, length - width, length, axis=dim)]
    slice x11 -> x0, other arithmetic: 9.25 us -> none  [padded_2(): last = lax.slice_in_dim(x, length - width, length, axis=dim)]
    div x1 -> x0, other arithmetic: 8.68 us -> none  [on_device(): column_sum = (here + below) / (pressure.shape[1] * lax.axis_size('cols'))]
  transfers between devices with their start and end apart: 37 -> 0, of which waited for: 35 -> 0; matrix products, arithmetic and copies ran while one was open for 1% -> 0% of each run, Pallas kernels for 0% -> 0%
where the time goes in v1:
time: 183 us
  Pallas kernels  171 us (93%)
  local copies, waits for them, and re-layouts  11.4 us (6%)
    pallas_call x1, Pallas kernels, on_device(): pl.pallas_call(functools.partial(kernel, counts, block), out_shape=[jax.S...  171 us
    unnamed x4, local copies, waits for them, and re-layouts  11.4 us

profile of v1, /device:TPU:24, one launch (start us, length us, event | category | flops | bytes accessed | tf_op | source)
XLA Modules:
  0.0 182.8 jit_solution(4025793201602655745)
XLA Ops:
  0.6 170.7 %shard_map.50 = (f32[16,8,128,128]{3,2,1,0:T(8,128)}, f32[16,8,128,128]{3,2,1,0:T(8,128)}) custom-call(f32[16,8,128,128]{3,2,1,0:T(8,128)} %p_hbm.1, f32[16,8,128,128]{3,2,1,0:T(8,128)} %e_hbm.1, f32[16,8,128,128]{3,2,1,0:T(8,128)} %c_hbm.1), custom_call_target="tpu_custom_call" | custom-call | tf_op jit(solution)/shard_map/pallas_call | solution.py:322
  171.4 0.0 copy-start
  171.4 8.0 %copy.7 = f32[16,8,128,128]{3,2,1,0:T(8,128)} copy(f32[16,8,128,128]{3,2,1,0:T(8,128)} %get-tuple-element.4) | data formatting | bytes 16777216
  179.4 0.0 copy-done
  179.4 3.4 %copy.8 = f32[16,8,128,128]{3,2,1,0:T(8,128)} copy(f32[16,8,128,128]{3,2,1,0:T(8,128)S(1)} %copy-done) | data formatting | bytes 16777216
Async XLA Ops:
  171.4 8.1 %copy-start = (f32[16,8,128,128]{3,2,1,0:T(8,128)S(1)}, f32[16,8,128,128]{3,2,1,0:T(8,128)}, u32[]{:S(2)}) copy-start(f32[16,8,128,128]{3,2,1,0:T(8,128)} %get-tuple-element.5) | copy-start | bytes 25165828

commit v2 on v1

--- a/solution.py
+++ b/solution.py
@@ -13,10 +13,12 @@
 AXES = ("rows", "cols", "slabs")
 
 
-def kernel(counts, block, p_hbm, e_hbm, c_hbm, sum_hbm, end_hbm, field, speed, z_out, z_in, sum_in, sum_out,
-           load_sem, x_send, x_recv, y_send, y_recv, z_send, z_recv, s_send, s_recv, store_sem):
+def kernel(counts, block, p_hbm, e_hbm, c_hbm, speed, end, field, z_out, z_in, sum_in, sum_out,
+           load_sem, x_send, x_recv, y_send, y_recv, z_send, z_recv, s_send, s_recv):
     ny, nx, nz, _ = block
-    chunk = 32 if nz % 32 == 0 else 8
+    parts = 2 if nz % (2 * PAD) == 0 else 1
+    half = nz // parts
+    chunk = 32 if half % 32 == 0 else PAD
     me = [lax.axis_index(axis) for axis in AXES]
     has = [(me[d] > 0, me[d] < counts[d] - 1) for d in range(3)]
 
@@ -30,6 +32,13 @@
 
     core_z = pl.ds(PAD, nz)
 
+    barrier = pltpu.get_barrier_semaphore()
+    for d in range(3):
+        for side, there in each(d):
+            @pl.when(there)
+            def _():
+                pl.semaphore_signal(barrier, inc=1, device_id=other(d, side), device_id_type=MESH)
+
     def load(which, y):
         hbm = (p_hbm, e_hbm, c_hbm)[which]
         dst = speed.at[y] if which == 2 else field.at[which, y + 1, pl.ds(1, nx), core_z, :]
@@ -43,9 +52,6 @@
             load(w, order(i)).start()
         return 0
 
-    lax.fori_loop(0, ny, functools.partial(loads, which=(0,)), 0)
-    lax.fori_loop(0, ny, functools.partial(loads, which=(1, 2)), 0)
-
     def x_copy(par, y, side, first=False):
         cell = nx - 1 if side else 0
         src = p_hbm.at[y, cell] if first else field.at[par, y + 1, cell + 1, core_z, :]
@@ -91,24 +97,20 @@
             send_sem=z_send.at[par, side, y], recv_sem=z_recv.at[par, side, y],
             device_id=other(2, side), device_id_type=MESH)
 
-    def s_copy(y):
-        return pltpu.make_async_remote_copy(
-            src_ref=sum_out.at[y], dst_ref=sum_in.at[y],
-            send_sem=s_send.at[y], recv_sem=s_recv.at[y],
+    def s_copy(y, part):
+        at = pl.ds(pl.multiple_of(part * half, PAD), half)
+        return pltpu.make_async_remote_copy(
+            src_ref=sum_out.at[y, at, :], dst_ref=sum_in.at[y, at, :],
+            send_sem=s_send.at[y, part], recv_sem=s_recv.at[y, part],
             device_id=other(1, 1), device_id_type=MESH)
 
-    def s_wait(y):
-        return pltpu.make_async_remote_copy(
-            src_ref=sum_in.at[y], dst_ref=sum_in.at[y],
-            send_sem=s_send.at[y], recv_sem=s_recv.at[y],
+    def s_wait(y, part):
+        here = sum_in.at[y, pl.ds(pl.multiple_of(part * half, PAD), half), :]
+        return pltpu.make_async_remote_copy(
+            src_ref=here, dst_ref=here,
+            send_sem=s_send.at[y, part], recv_sem=s_recv.at[y, part],
             device_id=other(1, 0), device_id_type=MESH)
 
-    barrier = pltpu.get_barrier_semaphore()
-    for d in range(3):
-        for side, there in each(d):
-            @pl.when(there)
-            def _():
-                pl.semaphore_signal(barrier, inc=1, device_id=other(d, side), device_id_type=MESH)
     peers = sum(there.astype(jnp.int32) for d in range(3) for _, there in each(d))
     pl.semaphore_wait(barrier, peers)
 
@@ -123,6 +125,8 @@
                 x_copy(0, order(i), side, True).start()
         return 0
     lax.fori_loop(0, ny, first_x, 0)
+    lax.fori_loop(0, ny, functools.partial(loads, which=(0,)), 0)
+    lax.fori_loop(0, ny, functools.partial(loads, which=(1, 2)), 0)
 
     lanes = block[3]
     def zero_x(side):
@@ -201,7 +205,7 @@
             def _():
                 z_copy(par, y, side).wait_send()
 
-    def cell(par, y, x, z):
+    def cell(par, y, x, z, final=False):
         def at(dy, dx, dz):
             return field[par, y + 1 + dy, x + 1 + dx, pl.ds(PAD + z + dz, chunk), :]
         middle = at(0, 0, 0)
@@ -209,7 +213,10 @@
                   - 6.0 * middle)
         before = field[1 - par, y + 1, x + 1, pl.ds(PAD + z, chunk), :]
         later = 2.0 * middle - before + speed[y, x, pl.ds(z, chunk), :] * spread
-        field[1 - par, y + 1, x + 1, pl.ds(PAD + z, chunk), :] = later
+        if final:
+            end[y, x, pl.ds(z, chunk), :] = later
+        else:
+            field[1 - par, y + 1, x + 1, pl.ds(PAD + z, chunk), :] = later
         return later
 
     def step(t, _):
@@ -245,57 +252,45 @@
 
     last = (STEPS - 1) % 2
 
-    def end_copy(y):
-        return pltpu.make_async_copy(field.at[1 - last, y + 1, pl.ds(1, nx), core_z, :], end_hbm.at[y], store_sem.at[0, y])
-
-    def sum_copy(y):
-        return pltpu.make_async_copy(speed.at[y], sum_hbm.at[y], store_sem.at[1, y])
-
     def last_row(i, _):
         y = order(i)
         arrive(last, y)
         sent(1 - last, y)
         for z in range(0, nz, chunk):
             def along(x, total):
-                total = total + cell(last, y, x, z)
+                total = total + cell(last, y, x, z, True)
                 speed[y, x, pl.ds(z, chunk), :] = total
                 return total
             total = lax.fori_loop(0, nx, along, jnp.zeros((chunk, lanes), jnp.float32))
-            @pl.when(jnp.logical_not(has[1][0]))
-            def _():
-                sum_out[y, pl.ds(z, chunk), :] = total
-        if counts[1] > 1:
-            @pl.when(jnp.logical_not(has[1][0]))
-            def _():
-                s_copy(y).start()
-        end_copy(y).start()
+            if counts[1] > 1:
+                @pl.when(jnp.logical_not(has[1][0]))
+                def _():
+                    sum_out[y, pl.ds(z, chunk), :] = total
+                    if (z + chunk) % half == 0:
+                        s_copy(y, z // half).start()
         return 0
     lax.fori_loop(0, ny, last_row, 0)
 
     scale = 1.0 / (nx * counts[1])
 
     def finish(i, _):
-        y = order(i)
+        y, part = order(i // parts), i % parts
+        places = [pl.ds(pl.multiple_of(part * half + z, PAD), chunk) for z in range(0, half, chunk)]
         if counts[1] > 1:
             @pl.when(has[1][0])
             def _():
-                s_wait(y).wait_recv()
+                s_wait(y, part).wait_recv()
                 @pl.when(has[1][1])
                 def _():
-                    for z in range(0, nz, chunk):
-                        at = pl.ds(z, chunk)
+                    for at in places:
                         sum_out[y, at, :] = sum_in[y, at, :] + speed[y, nx - 1, at, :]
-                    s_copy(y).start()
-        for z in range(0, nz, chunk):
-            at = pl.ds(z, chunk)
+                    s_copy(y, part).start()
+        for at in places:
             below = sum_in[y, at, :]
-            def along(x, _):
+            for x in range(nx):
                 speed[y, x, at, :] = (speed[y, x, at, :] + below) * scale
-                return 0
-            lax.fori_loop(0, nx, along, 0)
-        sum_copy(y).start()
-        return 0
-    lax.fori_loop(0, ny, finish, 0)
+        return 0
+    lax.fori_loop(0, ny * parts, finish, 0)
 
     def drain(i, _):
         y = order(i)
@@ -303,11 +298,23 @@
         if counts[1] > 1:
             @pl.when(has[1][1])
             def _():
-                s_copy(y).wait_send()
-        end_copy(y).wait()
-        sum_copy(y).wait()
+                for part in range(parts):
+                    s_copy(y, part).wait_send()
         return 0
     lax.fori_loop(0, ny, drain, 0)
+
+
+def write(rows, sum_ref, end_ref, sum_hbm, end_hbm, sem):
+    def copies(y):
+        return (pltpu.make_async_copy(sum_ref.at[y], sum_hbm.at[y], sem.at[0, y]),
+                pltpu.make_async_copy(end_ref.at[y], end_hbm.at[y], sem.at[1, y]))
+
+    for y in range(rows):
+        for copy in copies(y):
+            copy.start()
+    for y in range(rows):
+        for copy in copies(y):
+            copy.wait()
 
 
 def solution(mesh):
@@ -318,15 +325,15 @@
         ny, nx, nz, lanes = block
         f32 = jnp.float32
         anywhere = pl.BlockSpec(memory_space=pl.ANY)
+        inside = pl.BlockSpec(memory_space=pltpu.VMEM)
         dma = pltpu.SemaphoreType.DMA
-        return pl.pallas_call(
+        column_sum, pressure_end = pl.pallas_call(
             functools.partial(kernel, counts, block),
-            out_shape=[jax.ShapeDtypeStruct(block, f32)] * 2,
+            out_shape=[pltpu.VMEM(block, f32)] * 2,
             in_specs=[anywhere] * 3,
-            out_specs=[anywhere] * 2,
+            out_specs=[inside] * 2,
             scratch_shapes=[
                 pltpu.VMEM((2, ny + 2, nx + 2, nz + 2 * PAD, lanes), f32),
-                pltpu.VMEM((ny, nx, nz, lanes), f32),
                 pltpu.VMEM((2, 2, ny, nx, lanes), f32),
                 pltpu.VMEM((2, 2, ny, nx, lanes), f32),
                 pltpu.VMEM((ny, nz, lanes), f32),
@@ -335,13 +342,20 @@
                 dma((2, 2, ny)), dma((2, 2, ny)),
                 dma((2, 2)), dma((2, 2)),
                 dma((2, 2, ny)), dma((2, 2, ny)),
-                dma((ny,)), dma((ny,)),
-                dma((2, ny)),
+                dma((ny, 2)), dma((ny, 2)),
             ],
             compiler_params=pltpu.CompilerParams(
-                collective_id=0, has_side_effects=True, vmem_limit_bytes=60 * 1024 * 1024
+                collective_id=0, has_side_effects=True, vmem_limit_bytes=40 * 1024 * 1024
             ),
         )(pressure, earlier, speed_square)
+        return pl.pallas_call(
+            functools.partial(write, ny),
+            out_shape=[jax.ShapeDtypeStruct(block, f32)] * 2,
+            in_specs=[inside] * 2,
+            out_specs=[anywhere] * 2,
+            scratch_shapes=[dma((2, ny))],
+            compiler_params=pltpu.CompilerParams(vmem_limit_bytes=1024 * 1024),
+        )(column_sum, pressure_end)
 
     spec = P("rows", "cols", "slabs", None)
     return jax.shard_map(

time: 183 us -> 176 us (0.962)
  local copies, waits for them, and re-layouts: 11.4 us -> 0 us
  Pallas kernels: 171 us -> 175 us
    unnamed x4 -> x0, local copies, waits for them, and re-layouts: 11.4 us -> none
    pallas_call x1 -> x2, Pallas kernels: 171 us -> 175 us  [the longest x1 169 us: on_device(): pl.pallas_call(functools.partial(kernel, counts, block), out_shape=[pltpu...]
where the time goes in v2:
time: 176 us
  Pallas kernels  175 us (99%)
    pallas_call x1, Pallas kernels, on_device(): pl.pallas_call(functools.partial(kernel, counts, block), out_shape=[pltpu...  169 us
    pallas_call x1, Pallas kernels, on_device(): pl.pallas_call(functools.partial(write, ny), out_shape=[jax.ShapeDtypeStr...  6.08 us

profile of v2, /device:TPU:24, one launch (start us, length us, event | category | flops | bytes accessed | tf_op | source)
XLA Modules:
  0.0 175.8 jit_solution(13644551856554153795)
XLA Ops:
  0.6 169.1 %shard_map.50 = (f32[16,8,128,128]{3,2,1,0:T(8,128)S(1)}, f32[16,8,128,128]{3,2,1,0:T(8,128)S(1)}) custom-call(f32[16,8,128,128]{3,2,1,0:T(8,128)} %p_hbm.1, f32[16,8,128,128]{3,2,1,0:T(8,128)} %e_hbm.1, f32[16,8,128,128]{3,2,1,0:T(8,128)} %c_hbm.1), custom_call_target="tpu_custom_call" | custom-call | tf_op jit(solution)/shard_map/pallas_call | solution.py:330
  169.7 6.1 %shard_map.51 = (f32[16,8,128,128]{3,2,1,0:T(8,128)}, f32[16,8,128,128]{3,2,1,0:T(8,128)}) custom-call(f32[16,8,128,128]{3,2,1,0:T(8,128)S(1)} %get-tuple-element.4.sum_ref, f32[16,8,128,128]{3,2,1,0:T(8,128)S(1)} %get-tuple-element.5.end_ref), custom_call_target="tpu_custom_call" | custom-call | tf_op jit(solution)/shard_map/pallas_call | solution.py:351

commit v3 on v2

--- a/solution.py
+++ b/solution.py
@@ -13,10 +13,14 @@
 AXES = ("rows", "cols", "slabs")
 
 
+def pieces(nz):
+    return 4 if nz % (4 * PAD) == 0 else 1
+
+
 def kernel(counts, block, p_hbm, e_hbm, c_hbm, speed, end, field, z_out, z_in, sum_in, sum_out,
            load_sem, x_send, x_recv, y_send, y_recv, z_send, z_recv, s_send, s_recv):
     ny, nx, nz, _ = block
-    parts = 2 if nz % (2 * PAD) == 0 else 1
+    parts = pieces(nz)
     half = nz // parts
     chunk = 32 if half % 32 == 0 else PAD
     me = [lax.axis_index(axis) for axis in AXES]
@@ -342,7 +346,7 @@
                 dma((2, 2, ny)), dma((2, 2, ny)),
                 dma((2, 2)), dma((2, 2)),
                 dma((2, 2, ny)), dma((2, 2, ny)),
-                dma((ny, 2)), dma((ny, 2)),
+                dma((ny, pieces(nz))), dma((ny, pieces(nz))),
             ],
             compiler_params=pltpu.CompilerParams(
                 collective_id=0, has_side_effects=True, vmem_limit_bytes=40 * 1024 * 1024

time: 176 us -> 176 us (level)
  no operation moved by 1% of the time
where the time goes in v3:
time: 176 us
  Pallas kernels  176 us (100%)
    pallas_call x1, Pallas kernels, on_device(): pl.pallas_call(functools.partial(kernel, counts, block), out_shape=[pltpu...  169 us
    pallas_call x1, Pallas kernels, on_device(): pl.pallas_call(functools.partial(write, ny), out_shape=[jax.ShapeDtypeStr...  6.08 us

profile of v3, /device:TPU:24, one launch (start us, length us, event | category | flops | bytes accessed | tf_op | source)
XLA Modules:
  0.0 176.2 jit_solution(12980651525686340063)
XLA Ops:
  0.6 169.4 %shard_map.50 = (f32[16,8,128,128]{3,2,1,0:T(8,128)S(1)}, f32[16,8,128,128]{3,2,1,0:T(8,128)S(1)}) custom-call(f32[16,8,128,128]{3,2,1,0:T(8,128)} %p_hbm.1, f32[16,8,128,128]{3,2,1,0:T(8,128)} %e_hbm.1, f32[16,8,128,128]{3,2,1,0:T(8,128)} %c_hbm.1), custom_call_target="tpu_custom_call" | custom-call | tf_op jit(solution)/shard_map/pallas_call | solution.py:334
  170.1 6.1 %shard_map.51 = (f32[16,8,128,128]{3,2,1,0:T(8,128)}, f32[16,8,128,128]{3,2,1,0:T(8,128)}) custom-call(f32[16,8,128,128]{3,2,1,0:T(8,128)S(1)} %get-tuple-element.4.sum_ref, f32[16,8,128,128]{3,2,1,0:T(8,128)S(1)} %get-tuple-element.5.end_ref), custom_call_target="tpu_custom_call" | custom-call | tf_op jit(solution)/shard_map/pallas_call | solution.py:355
